TPU v7x, 32 devices: a whole 2x2x4 slice. The times are simulated.
32 devices in a mesh: shard: 4 (over y, x), tp: 8 (over z, core).
Axes of the slice: x: 2, y: 2, z: 4, core: 2. Of those that a mesh axis runs over, the one named last changes fastest.
Arguments:
- w_gate: float32 [5120, 17408], P('shard', 'tp'), may hold values from -0.125 to 0.125
- first_gate: float32 [5120, 17408], P('shard', 'tp'), may hold values from -0.078125 to 0.078125
- second_gate: float32 [5120, 17408], P('shard', 'tp'), may hold values from -0.078125 to 0.078125
- w_up: float32 [5120, 17408], P('shard', 'tp'), may hold values from -0.125 to 0.125
- first_up: float32 [5120, 17408], P('shard', 'tp'), may hold values from -0.078125 to 0.078125
- second_up: float32 [5120, 17408], P('shard', 'tp'), may hold values from -0.078125 to 0.078125
- norm_gain: float32 [5120], P('shard'), may hold values from 0.25 to 1.75
Outputs:
- serving_gate: bfloat16 [5120, 17408], P(None, 'tp')
- serving_up: bfloat16 [5120, 17408], P(None, 'tp')
- column_gate: float32 [17408], P('tp')
- column_up: float32 [17408], P('tp')
All inputs are finite; a program needn't handle non-finite values.
Results may differ from a plain program's by a relative error of at most 0.001.
Values may be sent and summed in bfloat16 or wider, within the bound.
A program may use at most 256 MiB of HBM per device.

v0:
```python
import functools

import jax
import jax.numpy as jnp
from jax import lax
from jax.experimental import pallas as pl
from jax.experimental.pallas import tpu as pltpu
from jax.sharding import PartitionSpec as P

learn_rate = 0.2
hold_rate = 0.8

LANES = 128
STEP = 32
MESH = pl.DeviceIdType.MESH


def plain(w_gate, first_gate, second_gate, w_up, first_up, second_up, norm_gain):
    hold_gate = hold_rate * first_gate + second_gate
    whole_gate = w_gate - learn_rate * hold_gate
    hold_up = hold_rate * first_up + second_up
    whole_up = w_up - learn_rate * hold_up
    whole_gained_gate = whole_gate * norm_gain[:, None]
    whole_gained_up = whole_up * norm_gain[:, None]
    total_gate, total_up = lax.psum(
        (
            jnp.sum(whole_gained_gate * whole_gained_gate, axis=0),
            jnp.sum(whole_gained_up * whole_gained_up, axis=0),
        ),
        "shard",
    )
    column_gate = jnp.sqrt(total_gate)
    column_up = jnp.sqrt(total_up)
    serving_gate, serving_up = (
        lax.all_gather((whole_gained_gate / column_gate).astype(jnp.bfloat16), "shard", axis=0, tiled=True),
        lax.all_gather((whole_gained_up / column_up).astype(jnp.bfloat16), "shard", axis=0, tiled=True),
    )
    return (serving_gate, serving_up, column_gate, column_up)


def cut(width, starts, most):
    tiles, sizes = width // LANES, []
    for size in starts:
        if tiles > size:
            sizes.append(size)
            tiles -= size
    while tiles > 0:
        sizes.append(min(most, tiles))
        tiles -= sizes[-1]
    chunks, at = [], 0
    for size in sizes:
        chunks.append((at * LANES, size * LANES))
        at += size
    return chunks


def kernel(
    chunks,
    rows,
    width,
    w_gate,
    first_gate,
    second_gate,
    w_up,
    first_up,
    second_up,
    gain,
    out_gate,
    out_up,
    columns,
    held,
    narrow,
    sums,
    load_sem,
    sum_send,
    sum_recv,
    own_send,
    own_recv,
    pass_send,
    pass_recv,
    local_sem,
):
    me = lax.axis_index("shard")
    row, column = me // 2, me % 2
    beside = row * 2 + (1 - column)
    above = (1 - row) * 2 + column
    across = (1 - row) * 2 + (1 - column)
    sources = ((w_gate, first_gate, second_gate), (w_up, first_up, second_up))
    outs = (out_gate, out_up)
    half = rows // 2

    def loads(k):
        which, first, size = chunks[k]
        return [
            pltpu.make_async_copy(
                ref.at[:, pl.ds(first, size)],
                held.at[k % 2, i, :, pl.ds(0, size)],
                load_sem.at[k % 2, i],
            )
            for i, ref in enumerate(sources[which])
        ]

    def send_sums(k):
        which, first, size = chunks[k]
        part = sums.at[me, :, pl.ds(which * width + first, size)]
        return [
            pltpu.make_async_remote_copy(
                src_ref=part,
                dst_ref=part,
                send_sem=sum_send.at[k, j],
                recv_sem=sum_recv.at[k, j],
                device_id={"shard": to},
                device_id_type=MESH,
            )
            for j, to in enumerate((beside, above, across))
        ]

    def send_own(k):
        which, first, size = chunks[k]
        return [
            pltpu.make_async_remote_copy(
                src_ref=narrow.at[:, pl.ds(which * width + first, size)],
                dst_ref=outs[which].at[pl.ds(me * rows, rows), pl.ds(first, size)],
                send_sem=own_send.at[k, j],
                recv_sem=own_recv.at[k, j],
                device_id={"shard": to},
                device_id_type=MESH,
            )
            for j, to in enumerate((beside, above))
        ]

    def keep_own(k):
        which, first, size = chunks[k]
        return pltpu.make_async_copy(
            narrow.at[:, pl.ds(which * width + first, size)],
            outs[which].at[pl.ds(me * rows, rows), pl.ds(first, size)],
            local_sem.at[k],
        )

    def send_on(k):
        which, first, size = chunks[k]
        copies = []
        for j, (origin, to) in enumerate(((above, beside), (beside, above))):
            part = outs[which].at[pl.ds(origin * rows + j * half, half), pl.ds(first, size)]
            copies.append(
                pltpu.make_async_remote_copy(
                    src_ref=part,
                    dst_ref=part,
                    send_sem=pass_send.at[k, j],
                    recv_sem=pass_recv.at[k, j],
                    device_id={"shard": to},
                    device_id_type=MESH,
                )
            )
        return copies

    for k in range(min(2, len(chunks))):
        for copy in loads(k):
            copy.start()
    barrier = pltpu.get_barrier_semaphore()
    for peer in (beside, above, across):
        pl.semaphore_signal(barrier, inc=1, device_id={"shard": peer}, device_id_type=MESH)

    for k, (which, first, size) in enumerate(chunks):
        slot, tiles = k % 2, size // LANES
        for copy in loads(k):
            copy.wait()

        def add_up(step, totals):
            here = pl.ds(pl.multiple_of(step * STEP, STEP), STEP)
            scale = gain[here, :]
            new = []
            for t in range(tiles):
                lanes = pl.ds(t * LANES, LANES)
                hold = hold_rate * held[slot, 1, here, lanes] + held[slot, 2, here, lanes]
                value = (held[slot, 0, here, lanes] - learn_rate * hold) * scale
                held[slot, 0, here, lanes] = value
                new.append(totals[t] + jnp.sum((value * value).reshape(STEP // 8, 8, LANES), axis=0))
            return tuple(new)

        totals = lax.fori_loop(
            0, rows // STEP, add_up, tuple(jnp.zeros((8, LANES), jnp.float32) for _ in range(tiles))
        )
        for t in range(tiles):
            sums[me, :, pl.ds(which * width + first + t * LANES, LANES)] = totals[t]
        if k == 0:
            pl.semaphore_wait(barrier, 3)
        exchange = send_sums(k)
        for copy in exchange:
            copy.start()
        for copy in exchange:
            copy.wait_recv()
        place = pl.ds(which * width + first, size)
        total = (sums[0, :, place] + sums[1, :, place]) + (sums[2, :, place] + sums[3, :, place])
        scale_of = jnp.sqrt(jnp.sum(total, axis=0, keepdims=True))
        columns[which : which + 1, pl.ds(first, size)] = scale_of
        inverse = 1.0 / scale_of

        def narrow_down(step, carry):
            here = pl.ds(pl.multiple_of(step * STEP, STEP), STEP)
            for t in range(tiles):
                value = held[slot, 0, here, pl.ds(t * LANES, LANES)]
                factor = inverse[:, t * LANES : (t + 1) * LANES]
                narrow[here, pl.ds(which * width + first + t * LANES, LANES)] = (value * factor).astype(jnp.bfloat16)
            return carry

        lax.fori_loop(0, rows // STEP, narrow_down, 0)
        for copy in send_own(k):
            copy.start()
        keep_own(k).start()
        if k + 2 < len(chunks):
            for copy in loads(k + 2):
                copy.start()

    for k in range(len(chunks)):
        arrived = send_own(k)
        onward = send_on(k)
        arrived[1].wait_recv()
        onward[0].start()
        arrived[0].wait_recv()
        onward[1].start()

    for k in range(len(chunks)):
        for copy in send_sums(k):
            copy.wait_send()
        for copy in send_own(k):
            copy.wait_send()
        keep_own(k).wait()
        for copy in send_on(k):
            copy.wait()


def per_device(w_gate, first_gate, second_gate, w_up, first_up, second_up, norm_gain):
    rows, width = w_gate.shape
    shards = lax.axis_size("shard")
    if shards != 4 or width % LANES or rows % (2 * STEP):
        return plain(w_gate, first_gate, second_gate, w_up, first_up, second_up, norm_gain)
    chunks = [(0, *chunk) for chunk in cut(width, (1, 2), 4)] + [(1, *chunk) for chunk in cut(width, (), 4)]
    most = max(size for _, _, size in chunks)
    count = len(chunks)
    gain = jnp.broadcast_to(norm_gain[:, None], (rows, LANES))
    anywhere = pl.BlockSpec(memory_space=pl.ANY)
    in_vmem = pl.BlockSpec(memory_space=pltpu.VMEM)
    dma = pltpu.SemaphoreType.DMA
    serving_gate, serving_up, columns = pl.pallas_call(
        functools.partial(kernel, chunks, rows, width),
        out_shape=(
            jax.ShapeDtypeStruct((shards * rows, width), jnp.bfloat16),
            jax.ShapeDtypeStruct((shards * rows, width), jnp.bfloat16),
            jax.ShapeDtypeStruct((2, width), jnp.float32),
        ),
        in_specs=[anywhere] * 6 + [in_vmem],
        out_specs=(anywhere, anywhere, in_vmem),
        scratch_shapes=[
            pltpu.VMEM((2, 3, rows, most), jnp.float32),
            pltpu.VMEM((rows, 2 * width), jnp.bfloat16),
            pltpu.VMEM((4, 8, 2 * width), jnp.float32),
            dma((2, 3)),
            dma((count, 3)),
            dma((count, 3)),
            dma((count, 2)),
            dma((count, 2)),
            dma((count, 2)),
            dma((count, 2)),
            dma((count,)),
        ],
        compiler_params=pltpu.CompilerParams(
            collective_id=0, has_side_effects=True, vmem_limit_bytes=48 * 1024 * 1024
        ),
    )(w_gate, first_gate, second_gate, w_up, first_up, second_up, gain)
    return (serving_gate, serving_up, columns[0], columns[1])


def solution(mesh):
    return jax.shard_map(
        per_device,
        mesh=mesh,
        in_specs=(
            P("shard", "tp"),
            P("shard", "tp"),
            P("shard", "tp"),
            P("shard", "tp"),
            P("shard", "tp"),
            P("shard", "tp"),
            P("shard"),
        ),
        out_specs=(P(None, "tp"), P(None, "tp"), P("tp"), P("tp")),
        check_vma=False,
    )
```

profile of v0, /device:TPU:0, one launch (start us, length us, event | category | flops | bytes accessed | tf_op | source)
XLA Modules:
  0.0 408.2 jit_solution(8909737863663012365)
XLA Ops:
  0.6 0.9 broadcast_in_dim.2.gain
  1.6 375.2 %shard_map.102 = (bf16[5120,2176]{1,0:T(8,128)(2,1)}, bf16[5120,2176]{1,0:T(8,128)(2,1)}, f32[2,2176]{1,0:T(2,128)S(1)}) custom-call(f32[1280,2176]{1,0:T(8,128)} %w_gate.1, f32[1280,2176]{1,0:T(8,128)} %first_gate.1, f32[1280,2176]{1,0:T(8,128)} %second_gate.1, f32[1280,2176]{1,0:T(8,128)} %w_up.1, f32[1280,2176]{1,0:T(8,128)} %first_up.1, ...), custom_call_target="tpu_custom_call" | custom-call | tf_op jit(solution)/shard_map/pallas_call | solution.py:245
  376.8 0.6 slice_reduce_fusion
  377.5 0.0 slice-start
  377.5 0.0 slice-start.1
  377.5 0.0 slice-start.2
  377.5 0.0 slice-start.3
  377.5 0.0 slice-start.4
  377.5 0.0 slice-start.5
  377.5 22.7 %copy.13 = bf16[5120,2176]{1,0:T(8,128)(2,1)} copy(bf16[5120,2176]{1,0:T(8,128)(2,1)} %get-tuple-element.16) | data formatting | bytes 44564480
  400.2 0.0 slice-done
  400.2 0.0 slice-done.1
  400.2 0.0 slice-done.2
  400.2 0.0 slice-done.3
  400.2 0.0 slice-done.4
  400.3 0.0 slice-done.5
  400.3 8.0 %copy.14 = bf16[5120,2176]{1,0:T(8,128)(2,1)} copy(bf16[5120,2176]{1,0:T(8,128)(2,1)S(1)} %bitcast.1) | data formatting | bytes 44564480
  (1 shorter events, 0.0 us)
Async XLA Ops:
  377.5 22.8 %slice-start = ((s8[22282240]{0:T(1024)(128)(4,1)}), s8[4194304]{0:T(1024)(128)(4,1)S(1)}, s32[]{:S(2)}) async-start(s8[22282240]{0:T(1024)(128)(4,1)} %bitcast), calls=%async_computation | async-start | bytes 8388608
  377.5 22.8 %slice-start.1 = ((s8[22282240]{0:T(1024)(128)(4,1)}), s8[4194304]{0:T(1024)(128)(4,1)S(1)}, s32[]{:S(2)}) async-start(s8[22282240]{0:T(1024)(128)(4,1)} %bitcast), calls=%async_computation.1 | async-start | bytes 8388608
  377.5 22.8 %slice-start.2 = ((s8[22282240]{0:T(1024)(128)(4,1)}), s8[4194304]{0:T(1024)(128)(4,1)S(1)}, s32[]{:S(2)}) async-start(s8[22282240]{0:T(1024)(128)(4,1)} %bitcast), calls=%async_computation.2 | async-start | bytes 8388608
  377.5 22.8 %slice-start.3 = ((s8[22282240]{0:T(1024)(128)(4,1)}), s8[4194304]{0:T(1024)(128)(4,1)S(1)}, s32[]{:S(2)}) async-start(s8[22282240]{0:T(1024)(128)(4,1)} %bitcast), calls=%async_computation.3 | async-start | bytes 8388608
  377.5 22.8 %slice-start.4 = ((s8[22282240]{0:T(1024)(128)(4,1)}), s8[4194304]{0:T(1024)(128)(4,1)S(1)}, s32[]{:S(2)}) async-start(s8[22282240]{0:T(1024)(128)(4,1)} %bitcast), calls=%async_computation.4 | async-start | bytes 8388608
  377.5 22.8 %slice-start.5 = ((s8[22282240]{0:T(1024)(128)(4,1)}), s8[1310720]{0:T(1024)(128)(4,1)S(1)}, s32[]{:S(2)}) async-start(s8[22282240]{0:T(1024)(128)(4,1)} %bitcast), calls=%async_computation.5 | async-start | bytes 2621440
where the time goes:
time: 408 us
  Pallas kernels  375 us (92%)
  local copies, waits for them, and re-layouts  32.3 us (8%)
    pallas_call x1, Pallas kernels, per_device(): pl.pallas_call(functools.partial(kernel, chunks, rows, width), out_shape=...  375 us
    unnamed x14, local copies, waits for them, and re-layouts  30.7 us

commit v1 on v0

v1 whole, which is shorter than its diff:
```python
import functools

import jax
import jax.numpy as jnp
from jax import lax
from jax.experimental import pallas as pl
from jax.experimental.pallas import tpu as pltpu
from jax.sharding import PartitionSpec as P

learn_rate = 0.2
hold_rate = 0.8

LANES = 128
STEP = 32
SLOTS = 3
TAIL = (4, 1)
MESH = pl.DeviceIdType.MESH
X_PAIRS = [(0, 1), (1, 0), (2, 3), (3, 2)]
Y_PAIRS = [(0, 2), (2, 0), (1, 3), (3, 1)]


def plain(w_gate, first_gate, second_gate, w_up, first_up, second_up, norm_gain):
    hold_gate = hold_rate * first_gate + second_gate
    whole_gate = w_gate - learn_rate * hold_gate
    hold_up = hold_rate * first_up + second_up
    whole_up = w_up - learn_rate * hold_up
    whole_gained_gate = whole_gate * norm_gain[:, None]
    whole_gained_up = whole_up * norm_gain[:, None]
    total_gate, total_up = lax.psum(
        (
            jnp.sum(whole_gained_gate * whole_gained_gate, axis=0),
            jnp.sum(whole_gained_up * whole_gained_up, axis=0),
        ),
        "shard",
    )
    column_gate = jnp.sqrt(total_gate)
    column_up = jnp.sqrt(total_up)
    serving_gate, serving_up = (
        lax.all_gather((whole_gained_gate / column_gate).astype(jnp.bfloat16), "shard", axis=0, tiled=True),
        lax.all_gather((whole_gained_up / column_up).astype(jnp.bfloat16), "shard", axis=0, tiled=True),
    )
    return (serving_gate, serving_up, column_gate, column_up)


def places(me):
    row, column = me // 2, me % 2
    beside = row * 2 + (1 - column)
    above = (1 - row) * 2 + column
    across = (1 - row) * 2 + (1 - column)
    return beside, above, across


def cut(tiles, starts, most):
    sizes = []
    for size in starts:
        if tiles > size:
            sizes.append(size)
            tiles -= size
    while tiles > 0:
        sizes.append(min(most, tiles))
        tiles -= sizes[-1]
    return sizes


def chunks_of(tiles):
    body = tiles - sum(TAIL)
    chunks = []
    for which, starts in ((0, (1, 2)), (1, ())):
        at = 0
        for size in cut(body, starts, 4):
            chunks.append((which, at * LANES, size * LANES, None))
            at += size
        for part, size in enumerate(TAIL):
            chunks.append((which, at * LANES, size * LANES, part))
            at += size
    return chunks


def exchange_kernel(
    chunks,
    rows,
    width,
    w_gate,
    first_gate,
    second_gate,
    w_up,
    first_up,
    second_up,
    gain_rows,
    main_gate,
    main_up,
    tail_gate_0,
    tail_gate_1,
    tail_up_0,
    tail_up_1,
    columns,
    held,
    narrow,
    sums,
    gain,
    load_sem,
    sum_send,
    sum_recv,
    own_send,
    own_recv,
    pass_send,
    pass_recv,
    local_sem,
):
    me = lax.axis_index("shard")
    beside, above, across = places(me)
    sources = ((w_gate, first_gate, second_gate), (w_up, first_up, second_up))
    mains = (main_gate, main_up)
    tails = ((tail_gate_0, tail_gate_1), (tail_up_0, tail_up_1))
    count = len(chunks)

    def block(which, origin, first, size):
        return mains[which].at[pl.ds(origin * rows, rows), pl.ds(first, size)]

    def loads(k):
        which, first, size, _ = chunks[k]
        return [
            pltpu.make_async_copy(
                ref.at[:, pl.ds(first, size)],
                held.at[k % SLOTS, i, :, pl.ds(0, size)],
                load_sem.at[k % SLOTS, i],
            )
            for i, ref in enumerate(sources[which])
        ]

    def send_sums(k):
        which, first, size, _ = chunks[k]
        part = sums.at[me, :, pl.ds(which * width + first, size)]
        return [
            pltpu.make_async_remote_copy(
                src_ref=part,
                dst_ref=part,
                send_sem=sum_send.at[k, j],
                recv_sem=sum_recv.at[k, j],
                device_id={"shard": to},
                device_id_type=MESH,
            )
            for j, to in enumerate((beside, above, across))
        ]

    def send_own(k):
        which, first, size, part = chunks[k]
        copies = []
        for j, to in enumerate((beside, above)):
            if part is not None and j == 1 - which:
                target = tails[which][part]
            else:
                target = block(which, me, first, size)
            copies.append(
                pltpu.make_async_remote_copy(
                    src_ref=narrow.at[:, pl.ds(which * width + first, size)],
                    dst_ref=target,
                    send_sem=own_send.at[k, j],
                    recv_sem=own_recv.at[k, j],
                    device_id={"shard": to},
                    device_id_type=MESH,
                )
            )
        return copies

    def keep_own(k):
        which, first, size, _ = chunks[k]
        return pltpu.make_async_copy(
            narrow.at[:, pl.ds(which * width + first, size)],
            block(which, me, first, size),
            local_sem.at[k],
        )

    def send_on(k):
        which, first, size, _ = chunks[k]
        part = block(which, (above, beside)[which], first, size)
        return pltpu.make_async_remote_copy(
            src_ref=part,
            dst_ref=part,
            send_sem=pass_send.at[k],
            recv_sem=pass_recv.at[k],
            device_id={"shard": (beside, above)[which]},
            device_id_type=MESH,
        )

    def add_up(k):
        which, first, size, _ = chunks[k]
        slot, tiles = k % SLOTS, size // LANES

        def body(step, totals):
            here = pl.ds(pl.multiple_of(step * STEP, STEP), STEP)
            scale = gain[here, :]
            new = []
            for t in range(tiles):
                lanes = pl.ds(t * LANES, LANES)
                hold = hold_rate * held[slot, 1, here, lanes] + held[slot, 2, here, lanes]
                value = (held[slot, 0, here, lanes] - learn_rate * hold) * scale
                held[slot, 0, here, lanes] = value
                new.append(totals[t] + jnp.sum((value * value).reshape(STEP // 8, 8, LANES), axis=0))
            return tuple(new)

        totals = lax.fori_loop(
            0, rows // STEP, body, tuple(jnp.zeros((8, LANES), jnp.float32) for _ in range(tiles))
        )
        for t in range(tiles):
            sums[me, :, pl.ds(which * width + first + t * LANES, LANES)] = totals[t]

    def narrow_down(k):
        which, first, size, _ = chunks[k]
        slot, tiles = k % SLOTS, size // LANES
        place = pl.ds(which * width + first, size)
        total = (sums[0, :, place] + sums[1, :, place]) + (sums[2, :, place] + sums[3, :, place])
        scale_of = jnp.sqrt(jnp.sum(total, axis=0, keepdims=True))
        columns[which : which + 1, pl.ds(first, size)] = scale_of
        inverse = 1.0 / scale_of

        def body(step, carry):
            here = pl.ds(pl.multiple_of(step * STEP, STEP), STEP)
            for t in range(tiles):
                value = held[slot, 0, here, pl.ds(t * LANES, LANES)]
                factor = inverse[:, t * LANES : (t + 1) * LANES]
                narrow[here, pl.ds(which * width + first + t * LANES, LANES)] = (value * factor).astype(jnp.bfloat16)
            return carry

        lax.fori_loop(0, rows // STEP, body, 0)

    def start(copies):
        for copy in copies:
            copy.start()

    start(loads(0))
    barrier = pltpu.get_barrier_semaphore()
    for peer in (beside, above, across):
        pl.semaphore_signal(barrier, inc=1, device_id={"shard": peer}, device_id_type=MESH)
    for b in range(rows // LANES):
        gain[pl.ds(b * LANES, LANES), :] = jnp.broadcast_to(gain_rows[b : b + 1, :], (LANES, LANES)).T

    for k in range(count + 1):
        if k < count:
            for copy in loads(k):
                copy.wait()
            if k == 0:
                for early in range(1, min(SLOTS, count)):
                    start(loads(early))
            add_up(k)
            if k == 0:
                pl.semaphore_wait(barrier, 3)
            start(send_sums(k))
        if k > 0:
            for copy in send_sums(k - 1):
                copy.wait_recv()
            narrow_down(k - 1)
            start(send_own(k - 1))
            keep_own(k - 1).start()
            if k - 1 + SLOTS < count:
                start(loads(k - 1 + SLOTS))

    for k, (which, _, _, part) in enumerate(chunks):
        arrived = send_own(k)
        if part is None:
            arrived[1 - which].wait_recv()
            send_on(k).start()

    for k, (which, _, _, part) in enumerate(chunks):
        arrived = send_own(k)
        arrived[which].wait_recv()
        if part is not None:
            arrived[1 - which].wait_recv()
        for copy in send_sums(k):
            copy.wait_send()
        for copy in arrived:
            copy.wait_send()
        keep_own(k).wait()
        if part is None:
            send_on(k).wait()


AHEAD = 4
RING = 8


def place_kernel(
    rows,
    width,
    body,
    parts,
    main_gate,
    main_up,
    tail_gate_0,
    tail_gate_1,
    tail_up_0,
    tail_up_1,
    columns_in,
    out_gate,
    out_up,
    columns,
    ring,
    load_sem,
    store_sem,
):
    me = lax.axis_index("shard")
    beside, above, across = places(me)
    columns[...] = columns_in[...]
    high = rows // parts
    jobs = []
    for which, (main, out, tails) in enumerate(
        ((main_gate, out_gate, (tail_gate_0, tail_gate_1)), (main_up, out_up, (tail_up_0, tail_up_1)))
    ):
        for origin, kind in ((me, 0), ((beside, above)[which], 0), ((above, beside)[which], 1), (across, 2)):
            for b in range(parts):
                here = pl.ds(origin * rows + b * high, high)
                pieces = []
                if kind == 0:
                    pieces.append((main.at[here, :], 0, width))
                else:
                    pieces.append((main.at[here, pl.ds(0, body)], 0, body))
                if kind == 1:
                    at = body
                    for tail in tails:
                        size = tail.shape[1]
                        pieces.append((tail.at[pl.ds(b * high, high), :], at, size))
                        at += size
                wide = body if kind == 2 else width
                jobs.append((pieces, out.at[here, pl.ds(0, wide)], wide))

    def load(i):
        slot = i % RING
        return [
            pltpu.make_async_copy(source, ring.at[slot, :, pl.ds(at, size)], load_sem.at[slot, j])
            for j, (source, at, size) in enumerate(jobs[i][0])
        ]

    def store(i):
        slot = i % RING
        _, target, wide = jobs[i]
        return pltpu.make_async_copy(ring.at[slot, :, pl.ds(0, wide)], target, store_sem.at[slot])

    count = len(jobs)
    for i in range(min(AHEAD, count)):
        for copy in load(i):
            copy.start()
    for i in range(count):
        later = i + AHEAD
        if later < count:
            if later >= RING:
                store(later - RING).wait()
            for copy in load(later):
                copy.start()
        for copy in load(i):
            copy.wait()
        store(i).start()
    for i in range(max(0, count - RING), count):
        store(i).wait()


def last_kernel(rows, first, from_gate, from_up, old_gate, old_up, out_gate, out_up, held, load_sem, store_sem):
    me = lax.axis_index("shard")
    _, _, across = places(me)
    size = from_gate.shape[1]
    ins = [
        pltpu.make_async_copy(ref, held.at[i], load_sem.at[i]) for i, ref in enumerate((from_gate, from_up))
    ]
    outs = [
        pltpu.make_async_copy(
            held.at[i], ref.at[pl.ds(across * rows, rows), pl.ds(first, size)], store_sem.at[i]
        )
        for i, ref in enumerate((out_gate, out_up))
    ]
    for copy in ins:
        copy.start()
    for one, two in zip(ins, outs):
        one.wait()
        two.start()
    for copy in outs:
        copy.wait()


def per_device(w_gate, first_gate, second_gate, w_up, first_up, second_up, norm_gain):
    rows, width = w_gate.shape
    shards = lax.axis_size("shard")
    if shards != 4 or width % LANES or rows % LANES or width // LANES < sum(TAIL) + 4:
        return plain(w_gate, first_gate, second_gate, w_up, first_up, second_up, norm_gain)
    chunks = chunks_of(width // LANES)
    body = width - sum(TAIL) * LANES
    most = max(size for _, _, size, _ in chunks)
    count = len(chunks)
    anywhere = pl.BlockSpec(memory_space=pl.ANY)
    in_vmem = pl.BlockSpec(memory_space=pltpu.VMEM)
    dma = pltpu.SemaphoreType.DMA
    whole = jax.ShapeDtypeStruct((shards * rows, width), jnp.bfloat16)
    two = jax.ShapeDtypeStruct((2, width), jnp.float32)
    tails = tuple(jax.ShapeDtypeStruct((rows, size * LANES), jnp.bfloat16) for size in TAIL)
    main_gate, main_up, tg0, tg1, tu0, tu1, columns = pl.pallas_call(
        functools.partial(exchange_kernel, chunks, rows, width),
        name="exchange",
        out_shape=(whole, whole, *tails, *tails, two),
        in_specs=[anywhere] * 6 + [in_vmem],
        out_specs=(anywhere,) * 6 + (in_vmem,),
        scratch_shapes=[
            pltpu.VMEM((SLOTS, 3, rows, most), jnp.float32),
            pltpu.VMEM((rows, 2 * width), jnp.bfloat16),
            pltpu.VMEM((4, 8, 2 * width), jnp.float32),
            pltpu.VMEM((rows, LANES), jnp.float32),
            dma((SLOTS, 3)),
            dma((count, 3)),
            dma((count, 3)),
            dma((count, 2)),
            dma((count, 2)),
            dma((count,)),
            dma((count,)),
            dma((count,)),
        ],
        compiler_params=pltpu.CompilerParams(
            collective_id=0, has_side_effects=True, vmem_limit_bytes=56 * 1024 * 1024
        ),
    )(w_gate, first_gate, second_gate, w_up, first_up, second_up, norm_gain.reshape(rows // LANES, LANES))
    on = [
        (lax.ppermute(gate, "shard", X_PAIRS), lax.ppermute(up, "shard", Y_PAIRS))
        for gate, up in ((tg0, tu0), (tg1, tu1))
    ]
    parts = 4
    out_gate, out_up, columns = pl.pallas_call(
        functools.partial(place_kernel, rows, width, body, parts),
        name="place",
        out_shape=(whole, whole, two),
        in_specs=[anywhere] * 6 + [in_vmem],
        out_specs=(anywhere, anywhere, in_vmem),
        scratch_shapes=[
            pltpu.VMEM((RING, rows // parts, width), jnp.bfloat16),
            dma((RING, 3)),
            dma((RING,)),
        ],
        compiler_params=pltpu.CompilerParams(vmem_limit_bytes=32 * 1024 * 1024),
        cost_estimate=pl.CostEstimate(flops=50_000_000, bytes_accessed=90_000_000, transcendentals=0),
    )(main_gate, main_up, tg0, tg1, tu0, tu1, columns)
    column_gate, column_up = columns[0], columns[1]
    first = body
    for (gate, up), size in zip(on, TAIL):
        out_gate, out_up = pl.pallas_call(
            functools.partial(last_kernel, rows, first),
            name="last",
            out_shape=(whole, whole),
            in_specs=[anywhere] * 4,
            out_specs=(anywhere, anywhere),
            scratch_shapes=[
                pltpu.VMEM((2, rows, size * LANES), jnp.bfloat16),
                dma((2,)),
                dma((2,)),
            ],
            input_output_aliases={2: 0, 3: 1},
        )(gate, up, out_gate, out_up)
        first += size * LANES
    return (out_gate, out_up, column_gate, column_up)


def solution(mesh):
    return jax.shard_map(
        per_device,
        mesh=mesh,
        in_specs=(
            P("shard", "tp"),
            P("shard", "tp"),
            P("shard", "tp"),
            P("shard", "tp"),
            P("shard", "tp"),
            P("shard", "tp"),
            P("shard"),
        ),
        out_specs=(P(None, "tp"), P(None, "tp"), P("tp"), P("tp")),
        check_vma=False,
    )
```

time: 408 us -> 385 us (0.944)
  local copies, waits for them, and re-layouts: 32.3 us -> 8.26 us
  starting transfers between devices: 0 us -> 4.12 us
    unnamed x14 -> x18, local copies, waits for them, and re-layouts: 30.7 us -> 7.62 us
    ppermute x0 -> x4, starting transfers between devices: none -> 4.12 us  [the longest x2 2.79 us: per_device(): lax.ppermute(gate, 'shard', X_PAIRS)]
    pallas_call x1 -> x4, Pallas kernels: 375 us -> 371 us  [the longest x1 340 us: per_device(): pl.pallas_call(functools.partial(exchange_kernel, chunks, rows, width), n...]
  transfers between devices with their start and end apart: 0 -> 4, of which waited for: 0 -> 0; matrix products, arithmetic and copies ran while one was open for 0% -> 0% of each run, Pallas kernels for 0% -> 8%
where the time goes in v1:
time: 385 us; the launch traced here: 384 us
  Pallas kernels  371 us (96%)
  local copies, waits for them, and re-layouts  8.26 us (2%)
  starting transfers between devices  4.12 us (1%)
    pallas_call x1, Pallas kernels, per_device(): pl.pallas_call(functools.partial(exchange_kernel, chunks, rows, width), n...  340 us
    pallas_call x1, Pallas kernels, per_device(): pl.pallas_call(functools.partial(place_kernel, rows, width, body, parts),...  26.7 us
  transfers between devices with their start and end apart: 4, of which 0 were waited for; matrix products, arithmetic and copies ran while one was open for 0% of the time, Pallas kernels for 8%

profile of v1, /device:TPU:0, one launch (start us, length us, event | category | flops | bytes accessed | tf_op | source)
XLA Modules:
  0.0 384.5 jit_solution(7044785060868612322)
XLA Ops:
  0.6 340.0 %exchange.1 = (bf16[5120,2176]{1,0:T(8,128)(2,1)}, bf16[5120,2176]{1,0:T(8,128)(2,1)}, bf16[1280,512]{1,0:T(8,128)(2,1)}, bf16[1280,128]{1,0:T(8,128)(2,1)}, bf1...) custom-call(f32[1280,2176]{1,0:T(8,128)} %w_gate.1, f32[1280,2176]{1,0:T(8,128)} %first_gate.1, ...), custom_call_target="tpu_custom_call" | custom-call | tf_op jit(solution)/shard_map/exchange/pallas_call | solution.py:393
  340.6 1.4 collective-permute-start.2
  342.0 0.7 collective-permute-start.3
  342.7 1.4 collective-permute-start
  344.1 0.7 collective-permute-start.1
  344.8 1.3 copy-done
  346.1 1.3 copy-done.1
  347.4 1.0 copy-done.2
  348.4 1.0 copy-done.3
  349.3 0.7 copy-done.4
  350.0 26.7 %place.1 = (bf16[5120,2176]{1,0:T(8,128)(2,1)}, bf16[5120,2176]{1,0:T(8,128)(2,1)}, f32[2,2176]{1,0:T(2,128)S(1)}) custom-call(bf16[5120,2176]{1,0:T(8,128)(2,1)} %get-tuple-element.22.main_gate, bf16[5120,2176]{1,0:T(8,128)(2,1)} %get-tuple-element.23.main_up, bf16[1280,512]{1,0:T(8,128)(2,1)S(1)} %copy-done.1, bf16[1280,128]{1,0:T(8,128)(2,1)S(1)} %copy-done.3, ...), custom_call_target="tpu_custom_call" | custom-call | flops 50000000 | bytes 90000000 | tf_op jit(solution)/shard_map/place/pallas_call | solution.py:422
  376.8 0.6 slice_reduce_fusion
  377.4 0.0 collective-permute-done.2.from_gate
  377.4 0.0 collective-permute-done.3.from_up
  377.4 1.1 copy-done.5
  378.5 0.4 copy-done.6
  378.9 2.8 last.2
  381.8 0.0 collective-permute-done.from_gate
  381.8 0.0 copy-start.7
  381.8 0.0 collective-permute-done.1.from_up
  381.8 0.0 copy-start.8
  381.8 0.7 copy-done.7
  382.5 0.1 copy-done.8
  382.6 1.8 last.3
  (7 shorter events, 0.0 us)
Async XLA Ops:
  340.6 36.8 %collective-permute-start.2 = (bf16[1280,512]{1,0:T(8,128)(2,1)}, bf16[1280,512]{1,0:T(8,128)(2,1)S(1)}, u32[]{:S(2)}, u32[]{:S(2)}) collective-permute-start(bf16[1280,512]{1,0:T(8,128)(2,1)} %get-tuple-element.20.tail_gate_0), channel_id=1, source_target_pairs={{0,8},{8,0},{16,24},{24,16},{1,9},{9,1},{17,25},{25,17},{2,10},{10... | collective-permute-start | bytes 3932168 | tf_op jit(solution)/shard_map/ppermute | solution.py:418
  342.0 35.4 %collective-permute-start.3 = (bf16[1280,512]{1,0:T(8,128)(2,1)}, bf16[1280,512]{1,0:T(8,128)(2,1)S(1)}, u32[]{:S(2)}, u32[]{:S(2)}) collective-permute-start(bf16[1280,512]{1,0:T(8,128)(2,1)} %get-tuple-element.21.tail_up_0), channel_id=1, source_target_pairs={{0,16},{16,0},{8,24},{24,8},{1,17},{17,1},{9,25},{25,9},{2,18},{18... | collective-permute-start | bytes 3932168 | tf_op jit(solution)/shard_map/ppermute | solution.py:418
  342.7 39.1 %collective-permute-start = (bf16[1280,128]{1,0:T(8,128)(2,1)}, bf16[1280,128]{1,0:T(8,128)(2,1)S(1)}, u32[]{:S(2)}, u32[]{:S(2)}) collective-permute-start(bf16[1280,128]{1,0:T(8,128)(2,1)} %get-tuple-element.18.tail_gate_1), channel_id=1, source_target_pairs={{0,8},{8,0},{16,24},{24,16},{1,9},{9,1},{17,25},{25,17},{2,10},{10... | collective-permute-start | bytes 983048 | tf_op jit(solution)/shard_map/ppermute | solution.py:418
  344.1 37.7 %collective-permute-start.1 = (bf16[1280,128]{1,0:T(8,128)(2,1)}, bf16[1280,128]{1,0:T(8,128)(2,1)S(1)}, u32[]{:S(2)}, u32[]{:S(2)}) collective-permute-start(bf16[1280,128]{1,0:T(8,128)(2,1)} %get-tuple-element.19.tail_up_1), channel_id=1, source_target_pairs={{0,16},{16,0},{8,24},{24,8},{1,17},{17,1},{9,25},{25,9},{2,18},{18... | collective-permute-start | bytes 983048 | tf_op jit(solution)/shard_map/ppermute | solution.py:418
  344.7 1.3 copy-start
  346.1 1.3 copy-start.1
  347.4 1.0 copy-start.2
  348.4 1.0 copy-start.3
  349.3 0.7 copy-start.4
  377.4 1.1 copy-start.5
  377.4 1.5 copy-start.6
  381.8 0.7 copy-start.7
  381.8 0.8 copy-start.8

commit v2 on v1

--- a/solution.py
+++ b/solution.py
@@ -13,6 +13,7 @@
 LANES = 128
 STEP = 32
 SLOTS = 3
+VMEM = 67043328
 TAIL = (4, 1)
 MESH = pl.DeviceIdType.MESH
 X_PAIRS = [(0, 1), (1, 0), (2, 3), (3, 2)]
@@ -65,7 +66,7 @@
 def chunks_of(tiles):
     body = tiles - sum(TAIL)
     chunks = []
-    for which, starts in ((0, (1, 2)), (1, ())):
+    for which, starts in ((0, (1, 1, 2)), (1, ())):
         at = 0
         for size in cut(body, starts, 4):
             chunks.append((which, at * LANES, size * LANES, None))
@@ -129,8 +130,7 @@
         ]
 
     def send_sums(k):
-        which, first, size, _ = chunks[k]
-        part = sums.at[me, :, pl.ds(which * width + first, size)]
+        part = sums.at[me, k, pl.ds(0, chunks[k][2] // LANES), :]
         return [
             pltpu.make_async_remote_copy(
                 src_ref=part,
@@ -143,10 +143,11 @@
             for j, to in enumerate((beside, above, across))
         ]
 
-    def send_own(k):
+    def send_own(k, links=(0, 1)):
         which, first, size, part = chunks[k]
         copies = []
-        for j, to in enumerate((beside, above)):
+        for j in links:
+            to = (beside, above)[j]
             if part is not None and j == 1 - which:
                 target = tails[which][part]
             else:
@@ -184,8 +185,7 @@
         )
 
     def add_up(k):
-        which, first, size, _ = chunks[k]
-        slot, tiles = k % SLOTS, size // LANES
+        slot, tiles = k % SLOTS, chunks[k][2] // LANES
 
         def body(step, totals):
             here = pl.ds(pl.multiple_of(step * STEP, STEP), STEP)
@@ -203,22 +203,22 @@
             0, rows // STEP, body, tuple(jnp.zeros((8, LANES), jnp.float32) for _ in range(tiles))
         )
         for t in range(tiles):
-            sums[me, :, pl.ds(which * width + first + t * LANES, LANES)] = totals[t]
+            sums[me, k, t : t + 1, :] = jnp.sum(totals[t], axis=0, keepdims=True)
 
     def narrow_down(k):
         which, first, size, _ = chunks[k]
         slot, tiles = k % SLOTS, size // LANES
-        place = pl.ds(which * width + first, size)
-        total = (sums[0, :, place] + sums[1, :, place]) + (sums[2, :, place] + sums[3, :, place])
-        scale_of = jnp.sqrt(jnp.sum(total, axis=0, keepdims=True))
-        columns[which : which + 1, pl.ds(first, size)] = scale_of
+        parts = [sums[i, k, 0:tiles, :] for i in range(4)]
+        scale_of = jnp.sqrt((parts[0] + parts[1]) + (parts[2] + parts[3]))
+        for t in range(tiles):
+            columns[which : which + 1, pl.ds(first + t * LANES, LANES)] = scale_of[t : t + 1, :]
         inverse = 1.0 / scale_of
 
         def body(step, carry):
             here = pl.ds(pl.multiple_of(step * STEP, STEP), STEP)
             for t in range(tiles):
                 value = held[slot, 0, here, pl.ds(t * LANES, LANES)]
-                factor = inverse[:, t * LANES : (t + 1) * LANES]
+                factor = inverse[t : t + 1, :]
                 narrow[here, pl.ds(which * width + first + t * LANES, LANES)] = (value * factor).astype(jnp.bfloat16)
             return carry
 
@@ -240,8 +240,9 @@
             for copy in loads(k):
                 copy.wait()
             if k == 0:
-                for early in range(1, min(SLOTS, count)):
-                    start(loads(early))
+                start(loads(1))
+            if k == 1:
+                start(loads(2))
             add_up(k)
             if k == 0:
                 pl.semaphore_wait(barrier, 3)
@@ -256,9 +257,8 @@
                 start(loads(k - 1 + SLOTS))
 
     for k, (which, _, _, part) in enumerate(chunks):
-        arrived = send_own(k)
         if part is None:
-            arrived[1 - which].wait_recv()
+            send_own(k, (1 - which,))[0].wait_recv()
             send_on(k).start()
 
     for k, (which, _, _, part) in enumerate(chunks):
@@ -353,24 +353,18 @@
         store(i).wait()
 
 
-def last_kernel(rows, first, from_gate, from_up, old_gate, old_up, out_gate, out_up, held, load_sem, store_sem):
+def last_kernel(rows, first, from_gate, from_up, old_gate, old_up, out_gate, out_up, store_sem):
     me = lax.axis_index("shard")
     _, _, across = places(me)
     size = from_gate.shape[1]
-    ins = [
-        pltpu.make_async_copy(ref, held.at[i], load_sem.at[i]) for i, ref in enumerate((from_gate, from_up))
-    ]
     outs = [
         pltpu.make_async_copy(
-            held.at[i], ref.at[pl.ds(across * rows, rows), pl.ds(first, size)], store_sem.at[i]
+            source, target.at[pl.ds(across * rows, rows), pl.ds(first, size)], store_sem.at[i]
         )
-        for i, ref in enumerate((out_gate, out_up))
+        for i, (source, target) in enumerate(((from_gate, out_gate), (from_up, out_up)))
     ]
-    for copy in ins:
+    for copy in outs:
         copy.start()
-    for one, two in zip(ins, outs):
-        one.wait()
-        two.start()
     for copy in outs:
         copy.wait()
 
@@ -386,6 +380,7 @@
     count = len(chunks)
     anywhere = pl.BlockSpec(memory_space=pl.ANY)
     in_vmem = pl.BlockSpec(memory_space=pltpu.VMEM)
+    in_hbm = pl.BlockSpec(memory_space=pltpu.HBM)
     dma = pltpu.SemaphoreType.DMA
     whole = jax.ShapeDtypeStruct((shards * rows, width), jnp.bfloat16)
     two = jax.ShapeDtypeStruct((2, width), jnp.float32)
@@ -399,7 +394,7 @@
         scratch_shapes=[
             pltpu.VMEM((SLOTS, 3, rows, most), jnp.float32),
             pltpu.VMEM((rows, 2 * width), jnp.bfloat16),
-            pltpu.VMEM((4, 8, 2 * width), jnp.float32),
+            pltpu.VMEM((4, count, 8, LANES), jnp.float32),
             pltpu.VMEM((rows, LANES), jnp.float32),
             dma((SLOTS, 3)),
             dma((count, 3)),
@@ -423,14 +418,14 @@
         functools.partial(place_kernel, rows, width, body, parts),
         name="place",
         out_shape=(whole, whole, two),
-        in_specs=[anywhere] * 6 + [in_vmem],
+        in_specs=[in_hbm] * 6 + [in_vmem],
         out_specs=(anywhere, anywhere, in_vmem),
         scratch_shapes=[
             pltpu.VMEM((RING, rows // parts, width), jnp.bfloat16),
             dma((RING, 3)),
             dma((RING,)),
         ],
-        compiler_params=pltpu.CompilerParams(vmem_limit_bytes=32 * 1024 * 1024),
+        compiler_params=pltpu.CompilerParams(vmem_limit_bytes=VMEM - 2 * sum(TAIL) * LANES * rows * 2 - 256 * 1024),
         cost_estimate=pl.CostEstimate(flops=50_000_000, bytes_accessed=90_000_000, transcendentals=0),
     )(main_gate, main_up, tg0, tg1, tu0, tu1, columns)
     column_gate, column_up = columns[0], columns[1]
@@ -440,14 +435,11 @@
             functools.partial(last_kernel, rows, first),
             name="last",
             out_shape=(whole, whole),
-            in_specs=[anywhere] * 4,
+            in_specs=[in_vmem, in_vmem, anywhere, anywhere],
             out_specs=(anywhere, anywhere),
-            scratch_shapes=[
-                pltpu.VMEM((2, rows, size * LANES), jnp.bfloat16),
-                dma((2,)),
-                dma((2,)),
-            ],
+            scratch_shapes=[dma((2,))],
             input_output_aliases={2: 0, 3: 1},
+            compiler_params=pltpu.CompilerParams(vmem_limit_bytes=1024 * 1024),
         )(gate, up, out_gate, out_up)
         first += size * LANES
     return (out_gate, out_up, column_gate, column_up)

time: 385 us -> 374 us (0.971)
  local copies, waits for them, and re-layouts: 8.26 us -> 1.45 us
  Pallas kernels: 371 us -> 366 us
    unnamed x18 -> x0, local copies, waits for them, and re-layouts: 7.62 us -> none
    pallas_call x1, Pallas kernels: 340 us -> 335 us  [per_device(): pl.pallas_call(functools.partial(exchange_kernel, chunks, rows, width), n...]
  transfers between devices with their start and end apart: 4 -> 4, of which waited for: 0 -> 2; matrix products, arithmetic and copies ran while one was open for 0% -> 0% of each run, Pallas kernels for 8% -> 8%
where the time goes in v2:
time: 374 us
  Pallas kernels  366 us (98%)
  starting transfers between devices  4.12 us (1%)
    pallas_call x1, Pallas kernels, per_device(): pl.pallas_call(functools.partial(exchange_kernel, chunks, rows, width), n...  335 us
    pallas_call x1, Pallas kernels, per_device(): pl.pallas_call(functools.partial(place_kernel, rows, width, body, parts),...  29 us
  transfers between devices with their start and end apart: 4, of which 2 were waited for; matrix products, arithmetic and copies ran while one was open for 0% of the time, Pallas kernels for 8%

profile of v2, /device:TPU:0, one launch (start us, length us, event | category | flops | bytes accessed | tf_op | source)
XLA Modules:
  0.0 374.0 jit_solution(6987309000383986484)
XLA Ops:
  0.6 335.0 %exchange.1 = (bf16[5120,2176]{1,0:T(8,128)(2,1)}, bf16[5120,2176]{1,0:T(8,128)(2,1)}, bf16[1280,512]{1,0:T(8,128)(2,1)}, bf16[1280,128]{1,0:T(8,128)(2,1)}, bf1...) custom-call(f32[1280,2176]{1,0:T(8,128)} %w_gate.1, f32[1280,2176]{1,0:T(8,128)} %first_gate.1, ...), custom_call_target="tpu_custom_call" | custom-call | tf_op jit(solution)/shard_map/exchange/pallas_call | solution.py:388
  335.6 1.5 collective-permute-start.2
  337.2 0.6 collective-permute-start.3
  337.7 1.4 collective-permute-start
  339.1 0.6 collective-permute-start.1
  339.8 29.0 %place.1 = (bf16[5120,2176]{1,0:T(8,128)(2,1)}, bf16[5120,2176]{1,0:T(8,128)(2,1)}, f32[2,2176]{1,0:T(2,128)}) custom-call(bf16[5120,2176]{1,0:T(8,128)(2,1)} %get-tuple-element.22.main_gate, bf16[5120,2176]{1,0:T(8,128)(2,1)} %get-tuple-element.23.main_up, bf16[1280,512]{1,0:T(8,128)(2,1)} %get-tuple-element.20.tail_gate_0, ...), custom_call_target="tpu_custom_call" | custom-call | flops 50000000 | bytes 90000000 | tf_op jit(solution)/shard_map/place/pallas_call | solution.py:417
  368.8 1.4 slice_reduce_fusion
  370.2 0.0 collective-permute-done.2.from_gate
  370.2 0.0 collective-permute-done.3.from_up
  370.2 1.5 last.2
  371.8 0.2 collective-permute-done.from_gate
  372.0 1.2 collective-permute-done.1.from_up
  373.2 0.8 last.3
Async XLA Ops:
  335.6 34.6 %collective-permute-start.2 = (bf16[1280,512]{1,0:T(8,128)(2,1)}, bf16[1280,512]{1,0:T(8,128)(2,1)S(1)}, u32[]{:S(2)}, u32[]{:S(2)}) collective-permute-start(bf16[1280,512]{1,0:T(8,128)(2,1)} %get-tuple-element.20.tail_gate_0), channel_id=1, source_target_pairs={{0,8},{8,0},{16,24},{24,16},{1,9},{9,1},{17,25},{25,17},{2,10},{10... | collective-permute-start | bytes 3932168 | tf_op jit(solution)/shard_map/ppermute | solution.py:413
  337.2 33.1 %collective-permute-start.3 = (bf16[1280,512]{1,0:T(8,128)(2,1)}, bf16[1280,512]{1,0:T(8,128)(2,1)S(1)}, u32[]{:S(2)}, u32[]{:S(2)}) collective-permute-start(bf16[1280,512]{1,0:T(8,128)(2,1)} %get-tuple-element.21.tail_up_0), channel_id=1, source_target_pairs={{0,16},{16,0},{8,24},{24,8},{1,17},{17,1},{9,25},{25,9},{2,18},{18... | collective-permute-start | bytes 3932168 | tf_op jit(solution)/shard_map/ppermute | solution.py:413
  337.7 34.3 %collective-permute-start = (bf16[1280,128]{1,0:T(8,128)(2,1)}, bf16[1280,128]{1,0:T(8,128)(2,1)S(1)}, u32[]{:S(2)}, u32[]{:S(2)}) collective-permute-start(bf16[1280,128]{1,0:T(8,128)(2,1)} %get-tuple-element.18.tail_gate_1), channel_id=1, source_target_pairs={{0,8},{8,0},{16,24},{24,16},{1,9},{9,1},{17,25},{25,17},{2,10},{10... | collective-permute-start | bytes 983048 | tf_op jit(solution)/shard_map/ppermute | solution.py:413
  339.1 34.1 %collective-permute-start.1 = (bf16[1280,128]{1,0:T(8,128)(2,1)}, bf16[1280,128]{1,0:T(8,128)(2,1)S(1)}, u32[]{:S(2)}, u32[]{:S(2)}) collective-permute-start(bf16[1280,128]{1,0:T(8,128)(2,1)} %get-tuple-element.19.tail_up_1), channel_id=1, source_target_pairs={{0,16},{16,0},{8,24},{24,8},{1,17},{17,1},{9,25},{25,9},{2,18},{18... | collective-permute-start | bytes 983048 | tf_op jit(solution)/shard_map/ppermute | solution.py:413

commit v3 on v2

--- a/solution.py
+++ b/solution.py
@@ -13,8 +13,9 @@
 LANES = 128
 STEP = 32
 SLOTS = 3
+LEAD = 1
 VMEM = 67043328
-TAIL = (4, 1)
+TAIL = (6, 1)
 MESH = pl.DeviceIdType.MESH
 X_PAIRS = [(0, 1), (1, 0), (2, 3), (3, 2)]
 Y_PAIRS = [(0, 2), (2, 0), (1, 3), (3, 1)]
@@ -99,6 +100,9 @@
     narrow,
     sums,
     gain,
+    early,
+    early_in,
+    early_out,
     load_sem,
     sum_send,
     sum_recv,
@@ -107,6 +111,10 @@
     pass_send,
     pass_recv,
     local_sem,
+    early_send,
+    early_recv,
+    early_pass,
+    early_keep,
 ):
     me = lax.axis_index("shard")
     beside, above, across = places(me)
@@ -114,6 +122,7 @@
     mains = (main_gate, main_up)
     tails = ((tail_gate_0, tail_gate_1), (tail_up_0, tail_up_1))
     count = len(chunks)
+    leads = lax.axis_index("tp") % 2 == LEAD
 
     def block(which, origin, first, size):
         return mains[which].at[pl.ds(origin * rows, rows), pl.ds(first, size)]
@@ -184,6 +193,57 @@
             device_id_type=MESH,
         )
 
+    def send_early(half):
+        here = pl.ds(half * (rows // 2), rows // 2)
+        return [
+            pltpu.make_async_remote_copy(
+                src_ref=early.at[here, :],
+                dst_ref=early_in.at[j, here, :],
+                send_sem=early_send.at[half, j],
+                recv_sem=early_recv.at[half, j],
+                device_id={"shard": to},
+                device_id_type=MESH,
+            )
+            for j, to in enumerate((beside, above))
+        ]
+
+    def early_on():
+        return pltpu.make_async_remote_copy(
+            src_ref=early_in.at[1],
+            dst_ref=early_in.at[2],
+            send_sem=early_pass.at[0],
+            recv_sem=early_pass.at[1],
+            device_id={"shard": beside},
+            device_id_type=MESH,
+        )
+
+    def keep_early():
+        _, first, size, _ = chunks[0]
+        return [
+            pltpu.make_async_copy(early_out.at[j], block(0, origin, first, size), early_keep.at[j])
+            for j, origin in enumerate((beside, above, across))
+        ]
+
+    def cast_early():
+        def body(step, carry):
+            here = pl.ds(pl.multiple_of(step * STEP, STEP), STEP)
+            early[here, :] = held[0, 0, here, pl.ds(0, LANES)].astype(jnp.bfloat16)
+            return carry
+
+        lax.fori_loop(0, rows // STEP, body, 0)
+
+    def scale_early():
+        inverse = 1.0 / columns[0:1, pl.ds(0, LANES)]
+
+        def body(step, carry):
+            here = pl.ds(pl.multiple_of(step * STEP, STEP), STEP)
+            for j in range(3):
+                value = early_in[j, here, :].astype(jnp.float32)
+                early_out[j, here, :] = (value * inverse).astype(jnp.bfloat16)
+            return carry
+
+        lax.fori_loop(0, rows // STEP, body, 0)
+
     def add_up(k):
         slot, tiles = k % SLOTS, chunks[k][2] // LANES
 
@@ -247,21 +307,74 @@
             if k == 0:
                 pl.semaphore_wait(barrier, 3)
             start(send_sums(k))
+            if k == 0:
+                pl.when(leads)(cast_early)
+            if k < 2:
+
+                @pl.when(leads)
+                def _():
+                    start(send_early(k))
+
         if k > 0:
             for copy in send_sums(k - 1):
                 copy.wait_recv()
             narrow_down(k - 1)
-            start(send_own(k - 1))
+            if k == 1:
+
+                @pl.when(jnp.logical_not(leads))
+                def _():
+                    start(send_own(0))
+
+            else:
+                start(send_own(k - 1))
             keep_own(k - 1).start()
             if k - 1 + SLOTS < count:
                 start(loads(k - 1 + SLOTS))
 
     for k, (which, _, _, part) in enumerate(chunks):
-        if part is None:
+        if k == 0:
+
+            @pl.when(leads)
+            def _():
+                for half in range(2):
+                    send_early(half)[1].wait_recv()
+                early_on().start()
+
+            @pl.when(jnp.logical_not(leads))
+            def _():
+                send_own(0, (1,))[0].wait_recv()
+                send_on(0).start()
+
+        elif part is None:
             send_own(k, (1 - which,))[0].wait_recv()
             send_on(k).start()
 
+    @pl.when(leads)
+    def _():
+        for half in range(2):
+            send_early(half)[0].wait_recv()
+        early_on().wait()
+        scale_early()
+        start(keep_early())
+        for half in range(2):
+            for copy in send_early(half):
+                copy.wait_send()
+        for copy in keep_early():
+            copy.wait()
+
+    @pl.when(jnp.logical_not(leads))
+    def _():
+        send_own(0, (0,))[0].wait_recv()
+        for copy in send_own(0):
+            copy.wait_send()
+        send_on(0).wait()
+
     for k, (which, _, _, part) in enumerate(chunks):
+        if k == 0:
+            for copy in send_sums(k):
+                copy.wait_send()
+            keep_own(k).wait()
+            continue
         arrived = send_own(k)
         arrived[which].wait_recv()
         if part is not None:
@@ -396,6 +509,9 @@
             pltpu.VMEM((rows, 2 * width), jnp.bfloat16),
             pltpu.VMEM((4, count, 8, LANES), jnp.float32),
             pltpu.VMEM((rows, LANES), jnp.float32),
+            pltpu.VMEM((rows, LANES), jnp.bfloat16),
+            pltpu.VMEM((3, rows, LANES), jnp.bfloat16),
+            pltpu.VMEM((3, rows, LANES), jnp.bfloat16),
             dma((SLOTS, 3)),
             dma((count, 3)),
             dma((count, 3)),
@@ -404,6 +520,10 @@
             dma((count,)),
             dma((count,)),
             dma((count,)),
+            dma((2, 2)),
+            dma((2, 2)),
+            dma((2,)),
+            dma((3,)),
         ],
         compiler_params=pltpu.CompilerParams(
             collective_id=0, has_side_effects=True, vmem_limit_bytes=56 * 1024 * 1024

time: 374 us -> 371 us (level)
  Pallas kernels: 366 us -> 350 us
  waiting for transfers between devices: 1.43 us -> 14.3 us
    pallas_call x1, Pallas kernels: 335 us -> 319 us  [per_device(): pl.pallas_call(functools.partial(exchange_kernel, chunks, rows, width), n...]
    ppermute x2, waiting for transfers between devices: 0.24 us -> 12.5 us  [per_device(): lax.ppermute(gate, 'shard', X_PAIRS)]
  transfers between devices with their start and end apart: 4 -> 4, of which waited for: 2 -> 4; matrix products, arithmetic and copies ran while one was open for 0% -> 0% of each run, Pallas kernels for 8% -> 8%
where the time goes in v3:
time: 371 us
  Pallas kernels  350 us (94%)
  waiting for transfers between devices  14.3 us (4%)
  starting transfers between devices  4.12 us (1%)
    pallas_call x1, Pallas kernels, per_device(): pl.pallas_call(functools.partial(exchange_kernel, chunks, rows, width), n...  319 us
    pallas_call x1, Pallas kernels, per_device(): pl.pallas_call(functools.partial(place_kernel, rows, width, body, parts),...  28.3 us
    ppermute x2, waiting for transfers between devices, per_device(): lax.ppermute(gate, 'shard', X_PAIRS)  12.5 us
  transfers between devices with their start and end apart: 4, of which 4 were waited for; matrix products, arithmetic and copies ran while one was open for 0% of the time, Pallas kernels for 8%

profile of v3, /device:TPU:0, one launch (start us, length us, event | category | flops | bytes accessed | tf_op | source)
XLA Modules:
  0.0 370.7 jit_solution(14368579395089867056)
XLA Ops:
  0.6 319.1 %exchange.1 = (bf16[5120,2176]{1,0:T(8,128)(2,1)}, bf16[5120,2176]{1,0:T(8,128)(2,1)}, bf16[1280,768]{1,0:T(8,128)(2,1)}, bf16[1280,128]{1,0:T(8,128)(2,1)}, bf1...) custom-call(f32[1280,2176]{1,0:T(8,128)} %w_gate.1, f32[1280,2176]{1,0:T(8,128)} %first_gate.1, ...), custom_call_target="tpu_custom_call" | custom-call | tf_op jit(solution)/shard_map/exchange/pallas_call | solution.py:501
  319.8 1.5 collective-permute-start.2
  321.3 0.6 collective-permute-start.3
  321.9 1.4 collective-permute-start
  323.3 0.6 collective-permute-start.1
  323.9 28.3 %place.1 = (bf16[5120,2176]{1,0:T(8,128)(2,1)}, bf16[5120,2176]{1,0:T(8,128)(2,1)}, f32[2,2176]{1,0:T(2,128)}) custom-call(bf16[5120,2176]{1,0:T(8,128)(2,1)} %get-tuple-element.22.main_gate, bf16[5120,2176]{1,0:T(8,128)(2,1)} %get-tuple-element.23.main_up, bf16[1280,768]{1,0:T(8,128)(2,1)} %get-tuple-element.20.tail_gate_0, ...), custom_call_target="tpu_custom_call" | custom-call | flops 50000000 | bytes 90000000 | tf_op jit(solution)/shard_map/place/pallas_call | solution.py:537
  352.2 1.4 slice_reduce_fusion
  353.6 11.8 %collective-permute-done.2.from_gate = bf16[1280,768]{1,0:T(8,128)(2,1)S(1)} collective-permute-done((bf16[1280,768]{1,0:T(8,128)(2,1)}, bf16[1280,768]{1,0:T(8,128)(2,1)S(1)}, u32[]{:S(2)}, u32[]{:S(2)}) %collective-permute-start.2) | collective-permute-done | bytes 1966112 | tf_op jit(solution)/shard_map/ppermute | solution.py:533
  365.4 0.9 collective-permute-done.3.from_up
  366.3 1.9 last.2
  368.3 0.7 collective-permute-done.from_gate
  369.0 0.9 collective-permute-done.1.from_up
  369.8 0.8 last.3
Async XLA Ops:
  319.8 45.7 %collective-permute-start.2 = (bf16[1280,768]{1,0:T(8,128)(2,1)}, bf16[1280,768]{1,0:T(8,128)(2,1)S(1)}, u32[]{:S(2)}, u32[]{:S(2)}) collective-permute-start(bf16[1280,768]{1,0:T(8,128)(2,1)} %get-tuple-element.20.tail_gate_0), channel_id=1, source_target_pairs={{0,8},{8,0},{16,24},{24,16},{1,9},{9,1},{17,25},{25,17},{2,10},{10... | collective-permute-start | bytes 5898248 | tf_op jit(solution)/shard_map/ppermute | solution.py:533
  321.3 45.0 %collective-permute-start.3 = (bf16[1280,768]{1,0:T(8,128)(2,1)}, bf16[1280,768]{1,0:T(8,128)(2,1)S(1)}, u32[]{:S(2)}, u32[]{:S(2)}) collective-permute-start(bf16[1280,768]{1,0:T(8,128)(2,1)} %get-tuple-element.21.tail_up_0), channel_id=1, source_target_pairs={{0,16},{16,0},{8,24},{24,8},{1,17},{17,1},{9,25},{25,9},{2,18},{18... | collective-permute-start | bytes 5898248 | tf_op jit(solution)/shard_map/ppermute | solution.py:533
  321.9 47.1 %collective-permute-start = (bf16[1280,128]{1,0:T(8,128)(2,1)}, bf16[1280,128]{1,0:T(8,128)(2,1)S(1)}, u32[]{:S(2)}, u32[]{:S(2)}) collective-permute-start(bf16[1280,128]{1,0:T(8,128)(2,1)} %get-tuple-element.18.tail_gate_1), channel_id=1, source_target_pairs={{0,8},{8,0},{16,24},{24,16},{1,9},{9,1},{17,25},{25,17},{2,10},{10... | collective-permute-start | bytes 983048 | tf_op jit(solution)/shard_map/ppermute | solution.py:533
  323.3 46.6 %collective-permute-start.1 = (bf16[1280,128]{1,0:T(8,128)(2,1)}, bf16[1280,128]{1,0:T(8,128)(2,1)S(1)}, u32[]{:S(2)}, u32[]{:S(2)}) collective-permute-start(bf16[1280,128]{1,0:T(8,128)(2,1)} %get-tuple-element.19.tail_up_1), channel_id=1, source_target_pairs={{0,16},{16,0},{8,24},{24,8},{1,17},{17,1},{9,25},{25,9},{2,18},{18... | collective-permute-start | bytes 983048 | tf_op jit(solution)/shard_map/ppermute | solution.py:533

commit v4 on v3

--- a/solution.py
+++ b/solution.py
@@ -14,6 +14,8 @@
 STEP = 32
 SLOTS = 3
 LEAD = 1
+HEAD = 256
+HOLD = 3
 VMEM = 67043328
 TAIL = (6, 1)
 MESH = pl.DeviceIdType.MESH
@@ -115,6 +117,7 @@
     early_recv,
     early_pass,
     early_keep,
+    first_sem,
 ):
     me = lax.axis_index("shard")
     beside, above, across = places(me)
@@ -136,6 +139,20 @@
                 load_sem.at[k % SLOTS, i],
             )
             for i, ref in enumerate(sources[which])
+        ]
+
+    cuts = (0, HEAD, (rows + HEAD) // 2, rows)
+
+    def first_loads(later):
+        low, high = ((0, HEAD), (HEAD, rows))[later]
+        _, first, size, _ = chunks[0]
+        return [
+            pltpu.make_async_copy(
+                ref.at[pl.ds(low, high - low), pl.ds(first, size)],
+                held.at[0, i, pl.ds(low, high - low), pl.ds(0, size)],
+                first_sem.at[later, i],
+            )
+            for i, ref in enumerate(sources[0])
         ]
 
     def send_sums(k):
@@ -193,14 +210,14 @@
             device_id_type=MESH,
         )
 
-    def send_early(half):
-        here = pl.ds(half * (rows // 2), rows // 2)
+    def send_early(part):
+        here = pl.ds(cuts[part], cuts[part + 1] - cuts[part])
         return [
             pltpu.make_async_remote_copy(
                 src_ref=early.at[here, :],
                 dst_ref=early_in.at[j, here, :],
-                send_sem=early_send.at[half, j],
-                recv_sem=early_recv.at[half, j],
+                send_sem=early_send.at[part, j],
+                recv_sem=early_recv.at[part, j],
                 device_id={"shard": to},
                 device_id_type=MESH,
             )
@@ -224,13 +241,13 @@
             for j, origin in enumerate((beside, above, across))
         ]
 
-    def cast_early():
+    def cast_early(low, high):
         def body(step, carry):
             here = pl.ds(pl.multiple_of(step * STEP, STEP), STEP)
             early[here, :] = held[0, 0, here, pl.ds(0, LANES)].astype(jnp.bfloat16)
             return carry
 
-        lax.fori_loop(0, rows // STEP, body, 0)
+        lax.fori_loop(low // STEP, high // STEP, body, 0)
 
     def scale_early():
         inverse = 1.0 / columns[0:1, pl.ds(0, LANES)]
@@ -244,7 +261,10 @@
 
         lax.fori_loop(0, rows // STEP, body, 0)
 
-    def add_up(k):
+    def zeros(k):
+        return tuple(jnp.zeros((8, LANES), jnp.float32) for _ in range(chunks[k][2] // LANES))
+
+    def add_up(k, low, high, totals):
         slot, tiles = k % SLOTS, chunks[k][2] // LANES
 
         def body(step, totals):
@@ -259,10 +279,10 @@
                 new.append(totals[t] + jnp.sum((value * value).reshape(STEP // 8, 8, LANES), axis=0))
             return tuple(new)
 
-        totals = lax.fori_loop(
-            0, rows // STEP, body, tuple(jnp.zeros((8, LANES), jnp.float32) for _ in range(tiles))
-        )
-        for t in range(tiles):
+        return lax.fori_loop(low // STEP, high // STEP, body, totals)
+
+    def keep_sums(k, totals):
+        for t in range(chunks[k][2] // LANES):
             sums[me, k, t : t + 1, :] = jnp.sum(totals[t], axis=0, keepdims=True)
 
     def narrow_down(k):
@@ -288,44 +308,69 @@
         for copy in copies:
             copy.start()
 
-    start(loads(0))
+    start(first_loads(0))
+    start(first_loads(1))
     barrier = pltpu.get_barrier_semaphore()
     for peer in (beside, above, across):
         pl.semaphore_signal(barrier, inc=1, device_id={"shard": peer}, device_id_type=MESH)
-    for b in range(rows // LANES):
-        gain[pl.ds(b * LANES, LANES), :] = jnp.broadcast_to(gain_rows[b : b + 1, :], (LANES, LANES)).T
+
+    def spread_gain(low, high):
+        for b in range(low // LANES, high // LANES):
+            gain[pl.ds(b * LANES, LANES), :] = jnp.broadcast_to(gain_rows[b : b + 1, :], (LANES, LANES)).T
+
+    spread_gain(0, HEAD)
 
     for k in range(count + 1):
         if k < count:
-            for copy in loads(k):
-                copy.wait()
             if k == 0:
-                start(loads(1))
-            if k == 1:
-                start(loads(2))
-            add_up(k)
-            if k == 0:
+                for copy in first_loads(0):
+                    copy.wait()
+                totals = add_up(0, 0, HEAD, zeros(0))
                 pl.semaphore_wait(barrier, 3)
-            start(send_sums(k))
-            if k == 0:
-                pl.when(leads)(cast_early)
-            if k < 2:
 
                 @pl.when(leads)
                 def _():
-                    start(send_early(k))
+                    cast_early(0, HEAD)
+                    start(send_early(0))
+
+                spread_gain(HEAD, rows)
+                for copy in first_loads(1):
+                    copy.wait()
+                start(loads(1))
+                keep_sums(0, add_up(0, HEAD, rows, totals))
+            else:
+                for copy in loads(k):
+                    copy.wait()
+                if k == 1:
+                    start(loads(2))
+                keep_sums(k, add_up(k, 0, rows, zeros(k)))
+            start(send_sums(k))
+            if k < 2:
+
+                @pl.when(leads)
+                def _():
+                    if k == 0:
+                        cast_early(HEAD, rows)
+                    start(send_early(k + 1))
 
         if k > 0:
             for copy in send_sums(k - 1):
                 copy.wait_recv()
             narrow_down(k - 1)
-            if k == 1:
+            if k == HOLD:
 
                 @pl.when(jnp.logical_not(leads))
                 def _():
-                    start(send_own(0))
-
-            else:
+                    for early_k in range(HOLD - 1):
+                        start(send_own(early_k))
+
+            if 1 < k < HOLD:
+
+                @pl.when(leads)
+                def _():
+                    start(send_own(k - 1))
+
+            if k >= HOLD:
                 start(send_own(k - 1))
             keep_own(k - 1).start()
             if k - 1 + SLOTS < count:
@@ -336,7 +381,7 @@
 
             @pl.when(leads)
             def _():
-                for half in range(2):
+                for half in range(3):
                     send_early(half)[1].wait_recv()
                 early_on().start()
 
@@ -351,12 +396,12 @@
 
     @pl.when(leads)
     def _():
-        for half in range(2):
+        for half in range(3):
             send_early(half)[0].wait_recv()
         early_on().wait()
         scale_early()
         start(keep_early())
-        for half in range(2):
+        for half in range(3):
             for copy in send_early(half):
                 copy.wait_send()
         for copy in keep_early():
@@ -485,7 +530,7 @@
 def per_device(w_gate, first_gate, second_gate, w_up, first_up, second_up, norm_gain):
     rows, width = w_gate.shape
     shards = lax.axis_size("shard")
-    if shards != 4 or width % LANES or rows % LANES or width // LANES < sum(TAIL) + 4:
+    if shards != 4 or width % LANES or rows % LANES or rows < 3 * HEAD or width // LANES < sum(TAIL) + 4:
         return plain(w_gate, first_gate, second_gate, w_up, first_up, second_up, norm_gain)
     chunks = chunks_of(width // LANES)
     body = width - sum(TAIL) * LANES
@@ -520,10 +565,11 @@
             dma((count,)),
             dma((count,)),
             dma((count,)),
-            dma((2, 2)),
-            dma((2, 2)),
+            dma((3, 2)),
+            dma((3, 2)),
             dma((2,)),
             dma((3,)),
+            dma((2, 3)),
         ],
         compiler_params=pltpu.CompilerParams(
             collective_id=0, has_side_effects=True, vmem_limit_bytes=56 * 1024 * 1024

time: 371 us -> 368 us (level)
  waiting for transfers between devices: 14.3 us -> 7.87 us
    ppermute x2, waiting for transfers between devices: 12.5 us -> 7.84 us  [per_device(): lax.ppermute(gate, 'shard', X_PAIRS)]
  transfers between devices with their start and end apart: 4 -> 4, of which waited for: 4 -> 2; matrix products, arithmetic and copies ran while one was open for 0% -> 0% of each run, Pallas kernels for 8% -> 8%
where the time goes in v4:
time: 368 us; the launch traced here: 367 us
  Pallas kernels  353 us (96%)
  waiting for transfers between devices  7.87 us (2%)
  starting transfers between devices  4.12 us (1%)
    pallas_call x1, Pallas kernels, per_device(): pl.pallas_call(functools.partial(exchange_kernel, chunks, rows, width), n...  322 us
    pallas_call x1, Pallas kernels, per_device(): pl.pallas_call(functools.partial(place_kernel, rows, width, body, parts),...  28.3 us
    ppermute x2, waiting for transfers between devices, per_device(): lax.ppermute(gate, 'shard', X_PAIRS)  7.84 us
  transfers between devices with their start and end apart: 4, of which 2 were waited for; matrix products, arithmetic and copies ran while one was open for 0% of the time, Pallas kernels for 8%

profile of v4, /device:TPU:0, one launch (start us, length us, event | category | flops | bytes accessed | tf_op | source)
XLA Modules:
  0.0 367.4 jit_solution(10289476111615026218)
XLA Ops:
  0.6 322.2 %exchange.1 = (bf16[5120,2176]{1,0:T(8,128)(2,1)}, bf16[5120,2176]{1,0:T(8,128)(2,1)}, bf16[1280,768]{1,0:T(8,128)(2,1)}, bf16[1280,128]{1,0:T(8,128)(2,1)}, bf1...) custom-call(f32[1280,2176]{1,0:T(8,128)} %w_gate.1, f32[1280,2176]{1,0:T(8,128)} %first_gate.1, ...), custom_call_target="tpu_custom_call" | custom-call | tf_op jit(solution)/shard_map/exchange/pallas_call | solution.py:546
  322.9 1.4 collective-permute-start.2
  324.2 0.7 collective-permute-start.3
  324.9 1.5 collective-permute-start
  326.4 0.6 collective-permute-start.1
  327.0 28.3 %place.1 = (bf16[5120,2176]{1,0:T(8,128)(2,1)}, bf16[5120,2176]{1,0:T(8,128)(2,1)}, f32[2,2176]{1,0:T(2,128)}) custom-call(bf16[5120,2176]{1,0:T(8,128)(2,1)} %get-tuple-element.22.main_gate, bf16[5120,2176]{1,0:T(8,128)(2,1)} %get-tuple-element.23.main_up, bf16[1280,768]{1,0:T(8,128)(2,1)} %get-tuple-element.20.tail_gate_0, ...), custom_call_target="tpu_custom_call" | custom-call | flops 50000000 | bytes 90000000 | tf_op jit(solution)/shard_map/place/pallas_call | solution.py:583
  355.3 1.4 slice_reduce_fusion
  356.7 6.3 %collective-permute-done.2.from_gate = bf16[1280,768]{1,0:T(8,128)(2,1)S(1)} collective-permute-done((bf16[1280,768]{1,0:T(8,128)(2,1)}, bf16[1280,768]{1,0:T(8,128)(2,1)S(1)}, u32[]{:S(2)}, u32[]{:S(2)}) %collective-permute-start.2) | collective-permute-done | bytes 1966112 | tf_op jit(solution)/shard_map/ppermute | solution.py:579
  363.0 0.0 collective-permute-done.3.from_up
  363.0 1.9 last.2
  365.0 1.6 collective-permute-done.from_gate
  366.5 0.0 collective-permute-done.1.from_up
  366.5 0.8 last.3
Async XLA Ops:
  322.9 40.2 %collective-permute-start.2 = (bf16[1280,768]{1,0:T(8,128)(2,1)}, bf16[1280,768]{1,0:T(8,128)(2,1)S(1)}, u32[]{:S(2)}, u32[]{:S(2)}) collective-permute-start(bf16[1280,768]{1,0:T(8,128)(2,1)} %get-tuple-element.20.tail_gate_0), channel_id=1, source_target_pairs={{0,8},{8,0},{16,24},{24,16},{1,9},{9,1},{17,25},{25,17},{2,10},{10... | collective-permute-start | bytes 5898248 | tf_op jit(solution)/shard_map/ppermute | solution.py:579
  324.2 38.8 %collective-permute-start.3 = (bf16[1280,768]{1,0:T(8,128)(2,1)}, bf16[1280,768]{1,0:T(8,128)(2,1)S(1)}, u32[]{:S(2)}, u32[]{:S(2)}) collective-permute-start(bf16[1280,768]{1,0:T(8,128)(2,1)} %get-tuple-element.21.tail_up_0), channel_id=1, source_target_pairs={{0,16},{16,0},{8,24},{24,8},{1,17},{17,1},{9,25},{25,9},{2,18},{18... | collective-permute-start | bytes 5898248 | tf_op jit(solution)/shard_map/ppermute | solution.py:579
  324.9 41.6 %collective-permute-start = (bf16[1280,128]{1,0:T(8,128)(2,1)}, bf16[1280,128]{1,0:T(8,128)(2,1)S(1)}, u32[]{:S(2)}, u32[]{:S(2)}) collective-permute-start(bf16[1280,128]{1,0:T(8,128)(2,1)} %get-tuple-element.18.tail_gate_1), channel_id=1, source_target_pairs={{0,8},{8,0},{16,24},{24,16},{1,9},{9,1},{17,25},{25,17},{2,10},{10... | collective-permute-start | bytes 983048 | tf_op jit(solution)/shard_map/ppermute | solution.py:579
  326.4 40.1 %collective-permute-start.1 = (bf16[1280,128]{1,0:T(8,128)(2,1)}, bf16[1280,128]{1,0:T(8,128)(2,1)S(1)}, u32[]{:S(2)}, u32[]{:S(2)}) collective-permute-start(bf16[1280,128]{1,0:T(8,128)(2,1)} %get-tuple-element.19.tail_up_1), channel_id=1, source_target_pairs={{0,16},{16,0},{8,24},{24,8},{1,17},{17,1},{9,25},{25,9},{2,18},{18... | collective-permute-start | bytes 983048 | tf_op jit(solution)/shard_map/ppermute | solution.py:579
